TPU v7x, 256 devices: a whole 4x4x8 slice. The times are simulated.
256 devices in a mesh: gx: 8 (over z), gy: 8 (over y, core), gz: 4 (over x).
Axes of the slice: x: 4, y: 4, z: 8, core: 2. Of those that a mesh axis runs over, the one named last changes fastest.
Arguments:
- density: float32 [64, 64, 512], P('gx', 'gy', 'gz'), may hold values from 0.5 to 2
- base_velocity: float32 [3, 64, 64, 512], P(None, 'gx', 'gy', 'gz'), may hold values from -0.4 to 0.4
- cells: int32 [3, 65536], P(None, ('gx', 'gy', 'gz')), may hold values from 0 to 511, as said below
- offsets: float32 [3, 65536], P(None, ('gx', 'gy', 'gz')), may hold values from 0 to 1
- target: float32 [3, 65536], P(None, ('gx', 'gy', 'gz')), may hold values from -0.4 to 0.4
- stiffness: float32 [65536], P(('gx', 'gy', 'gz')), may hold values from 0.01 to 0.1
- counts: int32 [256], P(('gx', 'gy', 'gz')), may hold values from 1 to 256, as said below
Outputs:
- forces: float32 [3, 65536], P(None, ('gx', 'gy', 'gz'))
Inputs may be any that keep to these rules, and one draw needn't show every extreme that they name: `cells`: each marker's cell lies inside the lattice block of the device that holds its slot. `counts`: some device holds exactly 256 live markers in every draw.
All inputs are finite; a program needn't handle non-finite values.
Results may differ from a plain program's by a relative error of at most 0.0001.
Values sent between devices are 32-bit elements; how exact they have to be, the bound alone decides.
A program may use at most 64 MiB of HBM per device.

v0:
```python
import jax
import jax.numpy as jnp
from jax import lax
from jax.sharding import Mesh
from jax.sharding import PartitionSpec as P

ITERS = 3
GY = ("gy_0", "gy_1")
GX_GY_GZ = ("gx", "gy_0", "gy_1", "gz")


def shifted(shard, axis, by):
    length = lax.axis_size(axis)
    return lax.ppermute(shard, axis, [(i, (i + by) % length) for i in range(length)])


def extended(cells, sides, width):
    for axis, dim in sides:
        count = lax.axis_size(axis)
        head = lax.slice_in_dim(cells, 0, width, axis=dim)
        tail = lax.slice_in_dim(cells, cells.shape[dim] - width, cells.shape[dim], axis=dim)
        cells = jnp.concatenate(
            [
                lax.ppermute(tail, axis, [(i, (i + 1) % count) for i in range(count)]),
                cells,
                lax.ppermute(head, axis, [((i + 1) % count, i) for i in range(count)]),
            ],
            axis=dim,
        )
    return cells


def one_axis_at_a_time(shard, axes):
    for axis in axes:
        shard = lax.psum(shard, axis)
    return shard


def moving_directions():
    listing = []
    for along_x in (-1, 0, 1):
        for along_y in (-1, 0, 1):
            for along_z in (-1, 0, 1):
                order = abs(along_x) + abs(along_y) + abs(along_z)
                if order == 1:
                    listing.append((along_x, along_y, along_z, 1.0 / 18.0))
                elif order == 2:
                    listing.append((along_x, along_y, along_z, 1.0 / 36.0))
    return listing


def delta_weights(fraction):

    def inner(radius):
        return (3.0 - 2.0 * radius + jnp.sqrt(1.0 + 4.0 * radius - 4.0 * radius * radius)) / 8.0

    def outer(radius):
        return (5.0 - 2.0 * radius - jnp.sqrt(-7.0 + 12.0 * radius - 4.0 * radius * radius)) / 8.0

    return jnp.stack(
        [outer(1.0 + fraction), inner(fraction), inner(1.0 - fraction), outer(2.0 - fraction)]
    )


def axis_rows(local, fraction, offset, extent):
    places = local[None, :] + jnp.arange(4, dtype=jnp.int32)[:, None] + offset
    hits = (places[:, :, None] == jnp.arange(extent, dtype=jnp.int32)[None, None, :]).astype(
        jnp.float32
    )
    return jnp.sum(delta_weights(fraction)[:, :, None] * hits, axis=0)


def make_tables(local, fractions, offset, extents):
    table_x = axis_rows(local[0], fractions[0], offset, extents[0]).T
    table_y = axis_rows(local[1], fractions[1], offset, extents[1]).T
    table_z = axis_rows(local[2], fractions[2], offset, extents[2])
    return (table_x, table_y, table_z)


def spread_dense(vector, tables):
    table_x, table_y, table_z = tables
    weighted = vector[:, None, None, :] * table_x[None, :, None, :] * table_y[None, None, :, :]
    return jnp.einsum("cxym,mz->cxyz", weighted, table_z, precision=lax.Precision.HIGHEST)


def interpolate_dense(field, tables):
    table_x, table_y, table_z = tables
    partial_rows = jnp.einsum("cxyz,mz->cxym", field, table_z, precision=lax.Precision.HIGHEST)
    return jnp.sum(partial_rows * (table_x[:, None, :] * table_y[None, :, :])[None], axis=(1, 2))


def surround(payload):
    stack = payload[None]
    tags = [(0, 0, 0)]
    pieces = [stack]
    grown = list(tags)
    for by in (-1, 1):
        pieces.append(shifted(stack, "gx", by))
        grown = grown + [(by, tag[1], tag[2]) for tag in tags]
    stack = jnp.concatenate(pieces, axis=0)
    tags = grown
    pieces = [stack]
    for by in (-1, 1):
        pieces.append(shifted(stack, GY, by))
        grown = grown + [(tag[0], by, tag[2]) for tag in tags]
    stack = jnp.concatenate(pieces, axis=0)
    tags = grown
    pieces = [stack]
    for by in (-1, 1):
        pieces.append(shifted(stack, "gz", by))
        grown = grown + [(tag[0], tag[1], by) for tag in tags]
    stack = jnp.concatenate(pieces, axis=0)
    return (stack, jnp.array(grown, dtype=jnp.int32))


def body(density, base_velocity, cells, offsets, target, stiffness, counts):
    size_x, size_y, size_z = density.shape
    capacity = cells.shape[1]
    anchor = jnp.stack(
        [lax.axis_index("gx") * size_x, lax.axis_index(GY) * size_y, lax.axis_index("gz") * size_z]
    )
    own_tables = make_tables(
        cells - anchor[:, None], offsets, 1, (size_x + 4, size_y + 4, size_z + 4)
    )
    live = (jnp.arange(capacity, dtype=jnp.int32) < counts[0]).astype(jnp.float32)
    scale = lax.rsqrt(density)
    stacked = jnp.concatenate([base_velocity, scale[None]], axis=0)
    fields = extended(stacked, (("gx", 1), (GY, 2), ("gz", 3)), 3)
    base_wide = fields[:3, 1 : size_x + 5, 1 : size_y + 5, 1 : size_z + 5]
    scale_wide = fields[3, 1 : size_x + 5, 1 : size_y + 5, 1 : size_z + 5]
    scale_full = fields[3]
    directions = moving_directions()
    block_sizes = jnp.array([size_x, size_y, size_z], dtype=jnp.int32)
    coordinates = (cells - anchor[:, None]).astype(jnp.float32)
    tables_all, tags = surround(jnp.concatenate([coordinates, offsets], axis=0))
    neighbour_local = (
        tables_all[:, :3].astype(jnp.int32) - (tags * block_sizes[None, :])[:, :, None]
    )
    neighbour_local = jnp.transpose(neighbour_local, (1, 0, 2)).reshape(3, -1)
    neighbour_fractions = jnp.transpose(tables_all[:, 3:], (1, 0, 2)).reshape(3, -1)
    neighbour_tables = make_tables(
        neighbour_local, neighbour_fractions, 2, (size_x + 6, size_y + 6, size_z + 6)
    )

    def spread_markers(vector):
        vectors_all, unused = surround(vector)
        flat_vectors = jnp.transpose(vectors_all, (1, 0, 2)).reshape(3, -1)
        return spread_dense(flat_vectors, neighbour_tables)

    def stream_wide(wide):
        post = jnp.zeros((3, size_x + 4, size_y + 4, size_z + 4), jnp.float32)
        for along_x, along_y, along_z, share in directions:
            piece = wide[
                :,
                1 - along_x : 5 - along_x + size_x,
                1 - along_y : 5 - along_y + size_y,
                1 - along_z : 5 - along_z + size_z,
            ]
            population = (
                3.0 * share * (along_x * piece[0] + along_y * piece[1] + along_z * piece[2])
            )
            post = post + jnp.stack(
                [along_x * population, along_y * population, along_z * population]
            )
        return scale_wide * (wide[:, 1 : size_x + 5, 1 : size_y + 5, 1 : size_z + 5] + post) * 0.5

    def apply(vector):
        wide = scale_full * spread_markers(vector)
        velocity_wide = stream_wide(wide)
        return live * (interpolate_dense(velocity_wide, own_tables) + stiffness * vector)

    def both_products(vector, image):
        return (
            one_axis_at_a_time(jnp.sum(vector * vector), GX_GY_GZ),
            one_axis_at_a_time(jnp.sum(vector * image), GX_GY_GZ),
        )

    right = live * (target - interpolate_dense(base_wide, own_tables))
    solution = jnp.zeros_like(right)
    residual = right
    image = apply(residual)
    norm_now, product = both_products(residual, image)
    alpha = norm_now / product
    direction = residual
    along = image
    for step in range(ITERS):
        solution = solution + alpha * direction
        residual = residual - alpha * along
        if step + 1 < ITERS:
            image = apply(residual)
            norm_next, product = both_products(residual, image)
            ratio = norm_next / norm_now
            alpha = norm_next / (product - ratio * norm_next / alpha)
            direction = residual + ratio * direction
            along = image + ratio * along
            norm_now = norm_next
    return solution


def solution(mesh):
    finer = Mesh(
        mesh.devices.reshape(mesh.shape["gx"], 4, 2, mesh.shape["gz"]), ("gx", "gy_0", "gy_1", "gz")
    )
    return jax.shard_map(
        body,
        mesh=finer,
        in_specs=(
            P("gx", GY, "gz"),
            P(None, "gx", GY, "gz"),
            P(None, GX_GY_GZ),
            P(None, GX_GY_GZ),
            P(None, GX_GY_GZ),
            P(GX_GY_GZ),
            P(GX_GY_GZ),
        ),
        out_specs=P(None, GX_GY_GZ),
        check_vma=False,
    )
```

profile of v0, /device:TPU:2, one launch (start us, length us, event | category | flops | bytes accessed | tf_op | source)
XLA Modules:
  0.0 327.5 jit_solution(7431941897793863222)
XLA Ops:
  1.5 1.9 collective-permute-start.13
  3.4 4.0 %collective-permute-start.12 = (f32[1,6,256]{2,1,0:T(8,128)S(1)}, f32[1,6,256]{2,1,0:T(8,128)S(1)}, u32[]{:S(2)}, u32[]{:S(2)}) collective-permute-start(f32[1,6,256]{2,1,0:T(8,128)S(1)} %maximum_bitcast_fusion), channel_id=1, source_target_pairs={{0,224},{32,0},{64,32},{96,64},{128,96},{160,128},{192,160},{224,1... | collective-permute-start | bytes 18440 | tf_op jit(solution)/shard_map/ppermute | solution.py:14
  9.1 3.2 collective-permute-start.1
  15.2 2.9 collective-permute-start.14
  18.2 1.5 collective-permute-done.14
  19.7 1.6 collective-permute-start.17
  22.9 2.9 collective-permute-start.3
  28.8 34.5 %select_reduce_fusion = f32[6912,134]{0,1:T(8,128)S(1)} fusion(f32[4,6912]{1,0:T(4,128)S(1)} %pad_maximum_fusion.5, s32[4,6912]{1,0:T(4,128)S(1)} %add_add_fusion), kind=kLoop, calls=%fused_computation.6 | loop fusion | flops 10188288 | bytes 3926016 | tf_op jit(solution)/shard_map/reduce_sum | solution.py:70
  63.6 1.0 select_reduce_fusion.1
  64.9 1.6 collective-permute-start.4
  68.0 8.6 %collective-permute-done.4 = f32[4,14,14,3]{3,2,1,0:T(8,128)S(1)} collective-permute-done((f32[4,14,14,3]{3,2,1,0:T(8,128)S(1)}, f32[4,14,14,3]{3,2,1,0:T(8,128)S(1)}, u32[]{:S(2)}, u32[]{:S(2)}) %collective-permute-start.4) | collective-permute-done | bytes 9440 | tf_op jit(solution)/shard_map/ppermute | solution.py:24
  79.0 3.2 collective-permute-start.6
  82.3 1.6 collective-permute-done.7
  83.9 2.9 collective-permute-start.8
  86.8 1.4 collective-permute-done.8
  89.4 1.6 collective-permute-start.11
  91.0 1.5 collective-permute-done.10
  92.5 2.2 collective-permute-done.11
  94.9 14.8 %fusion.15 = f32[3,14,14,134]{3,2,1,0:T(8,128)S(1)} fusion(f32[6912,134]{0,1:T(8,128)S(1)} %select_reduce_fusion, f32[14,6912]{1,0:T(8,128)S(1)} %bitcast.78, f32[3,14,6912]{2,1,0:T(8,128)S(1)} %broadcast_multiply_fusion.2, f32[14,14,134]{2,1,0:T(8,128)S(1)} %slice_bitcast_fusion), kind=kOutput, calls=%fused_computation.21 | convolution fusion | flops 6539466752 | bytes 5673344 | tf_op jit(solution)/shard_map/cxym,mz->cxyz/dot_general | solution.py:83
  113.8 1.7 fusion.31
  116.3 18.0 %all-reduce.2 = (f32[]{:T(128)}, f32[]{:T(128)}) all-reduce(f32[]{:T(128)} %get-tuple-element.13, f32[]{:T(128)} %get-tuple-element.12), channel_id=1, replica_groups=mesh['gx'=8,'gy_0'=4,'gy_1'=2,'gz'=4] {'gx'}, use_global_device_ids=true, to_apply=%region_5.0 | all-reduce | flops 2 | bytes 16 | tf_op jit(solution)/shard_map/psum | solution.py:35
  134.3 10.3 %all-reduce.8 = (f32[]{:T(128)}, f32[]{:T(128)}) all-reduce(f32[]{:T(128)} %get-tuple-element.18, f32[]{:T(128)} %get-tuple-element.19), channel_id=1, replica_groups=mesh['gx'=8,'gy_0'=4,'gy_1'=2,'gz'=4] {'gy_0'}, use_global_device_ids=true, to_apply=%region_6.0 | all-reduce | flops 2 | bytes 16 | tf_op jit(solution)/shard_map/psum | solution.py:35
  144.6 3.1 all-reduce.11
  147.7 11.8 %all-reduce.5 = (f32[]{:T(128)}, f32[]{:T(128)}) all-reduce(f32[]{:T(128)} %get-tuple-element.36, f32[]{:T(128)} %get-tuple-element.37), channel_id=1, replica_groups=mesh['gx'=8,'gy_0'=4,'gy_1'=2,'gz'=4] {'gz'}, use_global_device_ids=true, to_apply=%region_8.0 | all-reduce | flops 2 | bytes 16 | tf_op jit(solution)/shard_map/psum | solution.py:35
  160.9 3.2 collective-permute-start.18
  164.1 1.6 collective-permute-done.19
  165.7 2.9 collective-permute-start.20
  168.7 1.4 collective-permute-done.20
  170.2 2.2 collective-permute-start.23
  172.4 1.7 collective-permute-done.22
  174.5 17.1 %fusion.20 = f32[3,14,14,134]{3,2,1,0:T(8,128)S(1)} fusion(f32[6912,134]{0,1:T(8,128)} %copy-done, f32[3,14,6912]{2,1,0:T(8,128)S(1)} %broadcast_multiply_fusion.1, f32[14,6912]{1,0:T(8,128)S(1)} %bitcast.79, f32[14,14,134]{2,1,0:T(8,128)S(1)} %slice_bitcast_fusion), kind=kOutput, calls=%fused_computation.22 | convolution fusion | flops 6539466752 | bytes 5673344 | tf_op jit(solution)/shard_map/cxym,mz->cxyz/dot_general | solution.py:83
  195.8 1.7 fusion.32
  198.1 18.1 %all-reduce.1 = (f32[]{:T(128)}, f32[]{:T(128)}) all-reduce(f32[]{:T(128)} %get-tuple-element.11, f32[]{:T(128)} %get-tuple-element.10), channel_id=1, replica_groups=mesh['gx'=8,'gy_0'=4,'gy_1'=2,'gz'=4] {'gx'}, use_global_device_ids=true, to_apply=%region_19.0 | all-reduce | flops 2 | bytes 16 | tf_op jit(solution)/shard_map/psum | solution.py:35
  216.2 8.4 %all-reduce.7 = (f32[]{:T(128)}, f32[]{:T(128)}) all-reduce(f32[]{:T(128)} %get-tuple-element.16, f32[]{:T(128)} %get-tuple-element.17), channel_id=1, replica_groups=mesh['gx'=8,'gy_0'=4,'gy_1'=2,'gz'=4] {'gy_0'}, use_global_device_ids=true, to_apply=%region_20.0 | all-reduce | flops 2 | bytes 16 | tf_op jit(solution)/shard_map/psum | solution.py:35
  224.5 3.1 all-reduce.10
  227.6 11.5 %all-reduce.4 = (f32[]{:T(128)}, f32[]{:T(128)}) all-reduce(f32[]{:T(128)} %get-tuple-element.34, f32[]{:T(128)} %get-tuple-element.35), channel_id=1, replica_groups=mesh['gx'=8,'gy_0'=4,'gy_1'=2,'gz'=4] {'gz'}, use_global_device_ids=true, to_apply=%region_22.0 | all-reduce | flops 2 | bytes 16 | tf_op jit(solution)/shard_map/psum | solution.py:35
  243.9 3.2 collective-permute-start.24
  247.1 1.6 collective-permute-done.25
  248.7 2.9 collective-permute-start.26
  251.7 1.4 collective-permute-done.26
  253.2 2.2 collective-permute-start.29
  255.4 2.1 collective-permute-done.28
  257.8 16.9 %fusion.25 = f32[3,14,14,134]{3,2,1,0:T(8,128)S(1)} fusion(f32[6912,134]{0,1:T(8,128)} %copy-done, f32[3,14,6912]{2,1,0:T(8,128)S(1)} %broadcast_multiply_fusion, f32[14,6912]{1,0:T(8,128)S(1)} %bitcast.80, f32[14,14,134]{2,1,0:T(8,128)S(1)} %slice_bitcast_fusion), kind=kOutput, calls=%fused_computation.23 | convolution fusion | flops 6539466752 | bytes 5673344 | tf_op jit(solution)/shard_map/cxym,mz->cxyz/dot_general | solution.py:83
  278.8 1.7 fusion.33
  281.2 18.0 %all-reduce = (f32[]{:T(128)}, f32[]{:T(128)}) all-reduce(f32[]{:T(128)} %get-tuple-element.9, f32[]{:T(128)} %get-tuple-element.8), channel_id=1, replica_groups=mesh['gx'=8,'gy_0'=4,'gy_1'=2,'gz'=4] {'gx'}, use_global_device_ids=true, to_apply=%region_30.0 | all-reduce | flops 2 | bytes 16 | tf_op jit(solution)/shard_map/psum | solution.py:35
  299.2 8.9 %all-reduce.6 = (f32[]{:T(128)}, f32[]{:T(128)}) all-reduce(f32[]{:T(128)} %get-tuple-element.14, f32[]{:T(128)} %get-tuple-element.15), channel_id=1, replica_groups=mesh['gx'=8,'gy_0'=4,'gy_1'=2,'gz'=4] {'gy_0'}, use_global_device_ids=true, to_apply=%region_31.0 | all-reduce | flops 2 | bytes 16 | tf_op jit(solution)/shard_map/psum | solution.py:35
  308.1 3.1 all-reduce.9
  311.2 11.5 %all-reduce.3 = (f32[]{:T(128)}, f32[]{:T(128)}) all-reduce(f32[]{:T(128)} %get-tuple-element.32, f32[]{:T(128)} %get-tuple-element.33), channel_id=1, replica_groups=mesh['gx'=8,'gy_0'=4,'gy_1'=2,'gz'=4] {'gz'}, use_global_device_ids=true, to_apply=%region_33.0 | all-reduce | flops 2 | bytes 16 | tf_op jit(solution)/shard_map/psum | solution.py:35
  (157 shorter events, 31.5 us)
Async XLA Ops:
  1.5 13.6 %collective-permute-start.13 = (f32[1,6,256]{2,1,0:T(8,128)S(1)}, f32[1,6,256]{2,1,0:T(8,128)S(1)}, u32[]{:S(2)}, u32[]{:S(2)}) collective-permute-start(f32[1,6,256]{2,1,0:T(8,128)S(1)} %maximum_bitcast_fusion), channel_id=1, source_target_pairs={{0,32},{32,64},{64,96},{96,128},{128,160},{160,192},{192,224},{224... | collective-permute-start | bytes 18440 | tf_op jit(solution)/shard_map/ppermute | solution.py:14
  3.4 11.7 %collective-permute-start.12 = (f32[1,6,256]{2,1,0:T(8,128)S(1)}, f32[1,6,256]{2,1,0:T(8,128)S(1)}, u32[]{:S(2)}, u32[]{:S(2)}) collective-permute-start(f32[1,6,256]{2,1,0:T(8,128)S(1)} %maximum_bitcast_fusion), channel_id=1, source_target_pairs={{0,224},{32,0},{64,32},{96,64},{128,96},{160,128},{192,160},{224,1... | collective-permute-start | bytes 18440 | tf_op jit(solution)/shard_map/ppermute | solution.py:14
  9.0 12.9 %collective-permute-start = (f32[4,3,8,128]{3,2,1,0:T(8,128)S(1)}, f32[4,3,8,128]{3,2,1,0:T(8,128)S(1)}, u32[]{:S(2)}, u32[]{:S(2)}) collective-permute-start(f32[4,3,8,128]{3,2,1,0:T(8,128)S(1)} %get-tuple-element.221), channel_id=1, source_target_pairs={{0,32},{32,64},{64,96},{96,128},{128,160},{160,192},{192,224},{224... | collective-permute-start | bytes 147464 | tf_op jit(solution)/shard_map/ppermute | solution.py:24
  9.1 12.8 %collective-permute-start.1 = (f32[4,3,8,128]{3,2,1,0:T(8,128)S(1)}, f32[4,3,8,128]{3,2,1,0:T(8,128)S(1)}, u32[]{:S(2)}, u32[]{:S(2)}) collective-permute-start(f32[4,3,8,128]{3,2,1,0:T(8,128)S(1)} %get-tuple-element.222), channel_id=1, source_target_pairs={{32,0},{64,32},{96,64},{128,96},{160,128},{192,160},{224,192},{0,2... | collective-permute-start | bytes 147464 | tf_op jit(solution)/shard_map/ppermute | solution.py:26
  15.2 4.5 %collective-permute-start.15 = (f32[3,6,256]{2,1,0:T(8,128)S(1)}, f32[3,6,256]{2,1,0:T(8,128)S(1)}, u32[]{:S(2)}, u32[]{:S(2)}) collective-permute-start(f32[3,6,256]{2,1,0:T(8,128)S(1)} %pad_maximum_fusion.8), channel_id=1, source_target_pairs={{0,4},{4,8},{8,12},{12,16},{16,20},{20,24},{24,28},{28,0},{1,5},{5... | collective-permute-start | bytes 55304 | tf_op jit(solution)/shard_map/ppermute | solution.py:14
  15.2 4.5 %collective-permute-start.14 = (f32[3,6,256]{2,1,0:T(8,128)S(1)}, f32[3,6,256]{2,1,0:T(8,128)S(1)}, u32[]{:S(2)}, u32[]{:S(2)}) collective-permute-start(f32[3,6,256]{2,1,0:T(8,128)S(1)} %pad_maximum_fusion.8), channel_id=1, source_target_pairs={{0,28},{4,0},{8,4},{12,8},{16,12},{20,16},{24,20},{28,24},{1,29},{... | collective-permute-start | bytes 55304 | tf_op jit(solution)/shard_map/ppermute | solution.py:14
  19.7 6.2 %collective-permute-start.17 = (f32[9,6,256]{2,1,0:T(8,128)S(1)}, f32[9,6,256]{2,1,0:T(8,128)S(1)}, u32[]{:S(2)}, u32[]{:S(2)}) collective-permute-start(f32[9,6,256]{2,1,0:T(8,128)S(1)} %get-tuple-element.238), channel_id=1, source_target_pairs={{0,1},{1,2},{2,3},{3,0},{4,5},{5,6},{6,7},{7,4},{8,9},{9,10},{10,1... | collective-permute-start | bytes 165896 | tf_op jit(solution)/shard_map/ppermute | solution.py:14
  21.3 4.6 %collective-permute-start.16 = (f32[9,6,256]{2,1,0:T(8,128)S(1)}, f32[9,6,256]{2,1,0:T(8,128)S(1)}, u32[]{:S(2)}, u32[]{:S(2)}) collective-permute-start(f32[9,6,256]{2,1,0:T(8,128)S(1)} %get-tuple-element.238), channel_id=1, source_target_pairs={{0,3},{1,0},{2,1},{3,2},{4,7},{5,4},{6,5},{7,6},{8,11},{9,8},{10,9... | collective-permute-start | bytes 165896 | tf_op jit(solution)/shard_map/ppermute | solution.py:14
  22.9 41.7 %collective-permute-start.2 = (f32[4,14,3,128]{3,2,1,0:T(4,128)S(1)}, f32[4,14,3,128]{3,2,1,0:T(4,128)S(1)}, u32[]{:S(2)}, u32[]{:S(2)}) collective-permute-start(f32[4,14,3,128]{3,2,1,0:T(4,128)S(1)} %get-tuple-element.183), channel_id=1, source_target_pairs={{0,4},{4,8},{8,12},{12,16},{16,20},{20,24},{24,28},{28,0},{1,5},{5... | collective-permute-start | bytes 258056 | tf_op jit(solution)/shard_map/ppermute | solution.py:24
  22.9 41.7 %collective-permute-start.3 = (f32[4,14,3,128]{3,2,1,0:T(4,128)S(1)}, f32[4,14,3,128]{3,2,1,0:T(4,128)S(1)}, u32[]{:S(2)}, u32[]{:S(2)}) collective-permute-start(f32[4,14,3,128]{3,2,1,0:T(4,128)S(1)} %get-tuple-element.184), channel_id=1, source_target_pairs={{4,0},{8,4},{12,8},{16,12},{20,16},{24,20},{28,24},{0,28},{5,1},{9... | collective-permute-start | bytes 258056 | tf_op jit(solution)/shard_map/ppermute | solution.py:26
  25.9 38.7 %copy-start.1 = (f32[3,8,8,128]{3,2,1,0:T(8,128)S(1)}, f32[3,8,8,128]{3,2,1,0:T(8,128)}, u32[]{:S(2)}) copy-start(f32[3,8,8,128]{3,2,1,0:T(8,128)} %param.10) | copy-start | bytes 294916
  63.3 31.6 %copy-start = (f32[6912,134]{0,1:T(8,128)}, f32[6912,134]{0,1:T(8,128)S(1)}, u32[]{:S(2)}) copy-start(f32[6912,134]{0,1:T(8,128)S(1)} %select_reduce_fusion) | copy-start | bytes 11114500
  63.6 15.4 %copy-start.3 = (f32[3,256]{1,0:T(4,128)S(1)}, f32[3,256]{1,0:T(4,128)}, u32[]{:S(2)}) copy-start(f32[3,256]{1,0:T(4,128)} %param.13) | copy-start | bytes 9220
  64.9 11.7 %collective-permute-start.4 = (f32[4,14,14,3]{3,2,1,0:T(8,128)S(1)}, f32[4,14,14,3]{3,2,1,0:T(8,128)S(1)}, u32[]{:S(2)}, u32[]{:S(2)}) collective-permute-start(f32[4,14,14,3]{3,2,1,0:T(8,128)S(1)} %get-tuple-element.181), channel_id=1, source_target_pairs={{0,1},{1,2},{2,3},{3,0},{4,5},{5,6},{6,7},{7,4},{8,9},{9,10},{10,1... | collective-permute-start | bytes 28232 | tf_op jit(solution)/shard_map/ppermute | solution.py:24
  66.5 11.1 %collective-permute-start.5 = (f32[4,14,14,3]{3,2,1,0:T(8,128)S(1)}, f32[4,14,14,3]{3,2,1,0:T(8,128)S(1)}, u32[]{:S(2)}, u32[]{:S(2)}) collective-permute-start(f32[4,14,14,3]{3,2,1,0:T(8,128)S(1)} %get-tuple-element.182), channel_id=1, source_target_pairs={{1,0},{2,1},{3,2},{0,3},{5,4},{6,5},{7,6},{4,7},{9,8},{10,9},{11,1... | collective-permute-start | bytes 28232 | tf_op jit(solution)/shard_map/ppermute | solution.py:26
  79.0 4.9 %collective-permute-start.7 = (f32[1,3,256]{2,1,0:T(4,128)S(1)}, f32[1,3,256]{2,1,0:T(4,128)S(1)}, u32[]{:S(2)}, u32[]{:S(2)}) collective-permute-start(f32[1,3,256]{2,1,0:T(4,128)S(1)} %bitcast.81), channel_id=1, source_target_pairs={{0,32},{32,64},{64,96},{96,128},{128,160},{160,192},{192,224},{224... | collective-permute-start | bytes 9224 | tf_op jit(solution)/shard_map/ppermute | solution.py:14
  79.0 4.8 %collective-permute-start.6 = (f32[1,3,256]{2,1,0:T(4,128)S(1)}, f32[1,3,256]{2,1,0:T(4,128)S(1)}, u32[]{:S(2)}, u32[]{:S(2)}) collective-permute-start(f32[1,3,256]{2,1,0:T(4,128)S(1)} %bitcast.82), channel_id=1, source_target_pairs={{0,224},{32,0},{64,32},{96,64},{128,96},{160,128},{192,160},{224,1... | collective-permute-start | bytes 9224 | tf_op jit(solution)/shard_map/ppermute | solution.py:14
  83.9 4.4 %collective-permute-start.9 = (f32[3,3,256]{2,1,0:T(4,128)S(1)}, f32[3,3,256]{2,1,0:T(4,128)S(1)}, u32[]{:S(2)}, u32[]{:S(2)}) collective-permute-start(f32[3,3,256]{2,1,0:T(4,128)S(1)} %pad_maximum_fusion.9), channel_id=1, source_target_pairs={{0,4},{4,8},{8,12},{12,16},{16,20},{20,24},{24,28},{28,0},{1,5},{5... | collective-permute-start | bytes 27656 | tf_op jit(solution)/shard_map/ppermute | solution.py:14
  83.9 4.3 %collective-permute-start.8 = (f32[3,3,256]{2,1,0:T(4,128)S(1)}, f32[3,3,256]{2,1,0:T(4,128)S(1)}, u32[]{:S(2)}, u32[]{:S(2)}) collective-permute-start(f32[3,3,256]{2,1,0:T(4,128)S(1)} %pad_maximum_fusion.9), channel_id=1, source_target_pairs={{0,28},{4,0},{8,4},{12,8},{16,12},{20,16},{24,20},{28,24},{1,29},{... | collective-permute-start | bytes 27656 | tf_op jit(solution)/shard_map/ppermute | solution.py:14
  88.3 4.3 %collective-permute-start.10 = (f32[9,3,256]{2,1,0:T(4,128)S(1)}, f32[9,3,256]{2,1,0:T(4,128)S(1)}, u32[]{:S(2)}, u32[]{:S(2)}) collective-permute-start(f32[9,3,256]{2,1,0:T(4,128)S(1)} %get-tuple-element.250), channel_id=1, source_target_pairs={{0,3},{1,0},{2,1},{3,2},{4,7},{5,4},{6,5},{7,6},{8,11},{9,8},{10,9... | collective-permute-start | bytes 82952 | tf_op jit(solution)/shard_map/ppermute | solution.py:14
  89.4 5.4 %collective-permute-start.11 = (f32[9,3,256]{2,1,0:T(4,128)S(1)}, f32[9,3,256]{2,1,0:T(4,128)S(1)}, u32[]{:S(2)}, u32[]{:S(2)}) collective-permute-start(f32[9,3,256]{2,1,0:T(4,128)S(1)} %get-tuple-element.250), channel_id=1, source_target_pairs={{0,1},{1,2},{2,3},{3,0},{4,5},{5,6},{6,7},{7,4},{8,9},{9,10},{10,1... | collective-permute-start | bytes 82952 | tf_op jit(solution)/shard_map/ppermute | solution.py:14
  113.8 1.7 copy-start.2
  160.8 4.9 %collective-permute-start.19 = (f32[1,3,256]{2,1,0:T(4,128)S(1)}, f32[1,3,256]{2,1,0:T(4,128)S(1)}, u32[]{:S(2)}, u32[]{:S(2)}) collective-permute-start(f32[1,3,256]{2,1,0:T(4,128)S(1)} %bitcast.84), channel_id=1, source_target_pairs={{0,32},{32,64},{64,96},{96,128},{128,160},{160,192},{192,224},{224... | collective-permute-start | bytes 9224 | tf_op jit(solution)/shard_map/ppermute | solution.py:14
  160.9 4.8 %collective-permute-start.18 = (f32[1,3,256]{2,1,0:T(4,128)S(1)}, f32[1,3,256]{2,1,0:T(4,128)S(1)}, u32[]{:S(2)}, u32[]{:S(2)}) collective-permute-start(f32[1,3,256]{2,1,0:T(4,128)S(1)} %bitcast.85), channel_id=1, source_target_pairs={{0,224},{32,0},{64,32},{96,64},{128,96},{160,128},{192,160},{224,1... | collective-permute-start | bytes 9224 | tf_op jit(solution)/shard_map/ppermute | solution.py:14
  165.7 4.4 %collective-permute-start.21 = (f32[3,3,256]{2,1,0:T(4,128)S(1)}, f32[3,3,256]{2,1,0:T(4,128)S(1)}, u32[]{:S(2)}, u32[]{:S(2)}) collective-permute-start(f32[3,3,256]{2,1,0:T(4,128)S(1)} %pad_maximum_fusion.10), channel_id=1, source_target_pairs={{0,4},{4,8},{8,12},{12,16},{16,20},{20,24},{24,28},{28,0},{1,5},{5... | collective-permute-start | bytes 27656 | tf_op jit(solution)/shard_map/ppermute | solution.py:14
  165.7 4.3 %collective-permute-start.20 = (f32[3,3,256]{2,1,0:T(4,128)S(1)}, f32[3,3,256]{2,1,0:T(4,128)S(1)}, u32[]{:S(2)}, u32[]{:S(2)}) collective-permute-start(f32[3,3,256]{2,1,0:T(4,128)S(1)} %pad_maximum_fusion.10), channel_id=1, source_target_pairs={{0,28},{4,0},{8,4},{12,8},{16,12},{20,16},{24,20},{28,24},{1,29},{... | collective-permute-start | bytes 27656 | tf_op jit(solution)/shard_map/ppermute | solution.py:14
  170.1 4.0 %collective-permute-start.22 = (f32[9,3,256]{2,1,0:T(4,128)S(1)}, f32[9,3,256]{2,1,0:T(4,128)S(1)}, u32[]{:S(2)}, u32[]{:S(2)}) collective-permute-start(f32[9,3,256]{2,1,0:T(4,128)S(1)} %get-tuple-element.246), channel_id=1, source_target_pairs={{0,3},{1,0},{2,1},{3,2},{4,7},{5,4},{6,5},{7,6},{8,11},{9,8},{10,9... | collective-permute-start | bytes 82952 | tf_op jit(solution)/shard_map/ppermute | solution.py:14
  170.2 4.2 %collective-permute-start.23 = (f32[9,3,256]{2,1,0:T(4,128)S(1)}, f32[9,3,256]{2,1,0:T(4,128)S(1)}, u32[]{:S(2)}, u32[]{:S(2)}) collective-permute-start(f32[9,3,256]{2,1,0:T(4,128)S(1)} %get-tuple-element.246), channel_id=1, source_target_pairs={{0,1},{1,2},{2,3},{3,0},{4,5},{5,6},{6,7},{7,4},{8,9},{9,10},{10,1... | collective-permute-start | bytes 82952 | tf_op jit(solution)/shard_map/ppermute | solution.py:14
  243.8 4.9 %collective-permute-start.25 = (f32[1,3,256]{2,1,0:T(4,128)S(1)}, f32[1,3,256]{2,1,0:T(4,128)S(1)}, u32[]{:S(2)}, u32[]{:S(2)}) collective-permute-start(f32[1,3,256]{2,1,0:T(4,128)S(1)} %bitcast.93), channel_id=1, source_target_pairs={{0,32},{32,64},{64,96},{96,128},{128,160},{160,192},{192,224},{224... | collective-permute-start | bytes 9224 | tf_op jit(solution)/shard_map/ppermute | solution.py:14
  243.9 4.8 %collective-permute-start.24 = (f32[1,3,256]{2,1,0:T(4,128)S(1)}, f32[1,3,256]{2,1,0:T(4,128)S(1)}, u32[]{:S(2)}, u32[]{:S(2)}) collective-permute-start(f32[1,3,256]{2,1,0:T(4,128)S(1)} %bitcast.94), channel_id=1, source_target_pairs={{0,224},{32,0},{64,32},{96,64},{128,96},{160,128},{192,160},{224,1... | collective-permute-start | bytes 9224 | tf_op jit(solution)/shard_map/ppermute | solution.py:14
  248.7 4.4 %collective-permute-start.27 = (f32[3,3,256]{2,1,0:T(4,128)S(1)}, f32[3,3,256]{2,1,0:T(4,128)S(1)}, u32[]{:S(2)}, u32[]{:S(2)}) collective-permute-start(f32[3,3,256]{2,1,0:T(4,128)S(1)} %pad_maximum_fusion.11), channel_id=1, source_target_pairs={{0,4},{4,8},{8,12},{12,16},{16,20},{20,24},{24,28},{28,0},{1,5},{5... | collective-permute-start | bytes 27656 | tf_op jit(solution)/shard_map/ppermute | solution.py:14
  248.7 4.3 %collective-permute-start.26 = (f32[3,3,256]{2,1,0:T(4,128)S(1)}, f32[3,3,256]{2,1,0:T(4,128)S(1)}, u32[]{:S(2)}, u32[]{:S(2)}) collective-permute-start(f32[3,3,256]{2,1,0:T(4,128)S(1)} %pad_maximum_fusion.11), channel_id=1, source_target_pairs={{0,28},{4,0},{8,4},{12,8},{16,12},{20,16},{24,20},{28,24},{1,29},{... | collective-permute-start | bytes 27656 | tf_op jit(solution)/shard_map/ppermute | solution.py:14
  253.1 4.3 %collective-permute-start.28 = (f32[9,3,256]{2,1,0:T(4,128)S(1)}, f32[9,3,256]{2,1,0:T(4,128)S(1)}, u32[]{:S(2)}, u32[]{:S(2)}) collective-permute-start(f32[9,3,256]{2,1,0:T(4,128)S(1)} %get-tuple-element.242), channel_id=1, source_target_pairs={{0,3},{1,0},{2,1},{3,2},{4,7},{5,4},{6,5},{7,6},{8,11},{9,8},{10,9... | collective-permute-start | bytes 82952 | tf_op jit(solution)/shard_map/ppermute | solution.py:14
  253.2 4.5 %collective-permute-start.29 = (f32[9,3,256]{2,1,0:T(4,128)S(1)}, f32[9,3,256]{2,1,0:T(4,128)S(1)}, u32[]{:S(2)}, u32[]{:S(2)}) collective-permute-start(f32[9,3,256]{2,1,0:T(4,128)S(1)} %get-tuple-element.242), channel_id=1, source_target_pairs={{0,1},{1,2},{2,3},{3,0},{4,5},{5,6},{6,7},{7,4},{8,9},{9,10},{10,1... | collective-permute-start | bytes 82952 | tf_op jit(solution)/shard_map/ppermute | solution.py:14
where the time goes:
time: 333 us; the launch traced here: 328 us
  blocking collectives  126 us (38%)
  other arithmetic  60.4 us (18%)
  matrix products  54.6 us (16%)
  starting transfers between devices  45.5 us (14%)
  waiting for transfers between devices  28.1 us (8%)
  between operations  11.7 us (4%)
    psum x12, blocking collectives, one_axis_at_a_time(): shard = lax.psum(shard, axis)  126 us
    dot_general x3, matrix products, spread_dense(): jnp.einsum('cxym,mz->cxyz', weighted, table_z, precision=lax.Precision.HI...  48.7 us
    ppermute x24, starting transfers between devices, shifted(): lax.ppermute(shard, axis, [(i, (i + by) % length) for i in range(length)])  37.1 us
    reduce_sum x6, other arithmetic, axis_rows(): return jnp.sum(delta_weights(fraction)[:, :, None] * hits, axis=0)  37 us
    ppermute x24, waiting for transfers between devices, shifted(): lax.ppermute(shard, axis, [(i, (i + by) % length) for i in range(length)])  18.6 us
    ppermute x3, waiting for transfers between devices, extended(): lax.ppermute(tail, axis, [(i, (i + 1) % count) for i in range(count)])  8.6 us
    mul x15, other arithmetic, stream_wide(): 3.0 * share * (along_x * piece[0] + along_y * piece[1] + along_z * piece[2])  7.43 us
    ppermute x3, starting transfers between devices, extended(): lax.ppermute(head, axis, [((i + 1) % count, i) for i in range(count)])  6.7 us
  transfers between devices with their start and end apart: 30, of which 15 were waited for; matrix products, arithmetic and copies ran while one was open for 14% of the time, Pallas kernels for 0%

commit v1 on v0

--- a/solution.py
+++ b/solution.py
@@ -32,7 +32,7 @@
 
 def one_axis_at_a_time(shard, axes):
     for axis in axes:
-        shard = lax.psum(shard, axis)
+        shard = jnp.sum(lax.all_gather(shard, axis), axis=0)
     return shard
 
 

time: 333 us -> 375 us (1.13)
  local copies, waits for them, and re-layouts: 1.68 us -> 36.4 us
  other arithmetic: 60.4 us -> 75.1 us
  blocking collectives: 126 us -> 118 us
    psum x12 -> x0, blocking collectives: 126 us -> none  [one_axis_at_a_time(): shard = lax.psum(shard, axis)]
    unnamed x0 -> x12, blocking collectives: none -> 118 us
    unnamed x27 -> x85, local copies, waits for them, and re-layouts: 0.16 us -> 34.9 us
    reduce_sum x0 -> x24, other arithmetic: none -> 14.8 us  [one_axis_at_a_time(): shard = jnp.sum(lax.all_gather(shard, axis), axis=0)]
  transfers between devices with their start and end apart: 30 -> 30, of which waited for: 15 -> 15; matrix products, arithmetic and copies ran while one was open for 14% -> 12% of each run, Pallas kernels for 0% -> 0%
where the time goes in v1:
time: 375 us; the launch traced here: 369 us
  blocking collectives  118 us (31%)
  other arithmetic  75.1 us (20%)
  matrix products  54.4 us (15%)
  starting transfers between devices  45.8 us (12%)
  local copies, waits for them, and re-layouts  36.4 us (10%)
  waiting for transfers between devices  28 us (7%)
  between operations  11.7 us (3%)
    unnamed x12, blocking collectives  118 us
    dot_general x3, matrix products, spread_dense(): jnp.einsum('cxym,mz->cxyz', weighted, table_z, precision=lax.Precision.HI...  48.5 us
    ppermute x24, starting transfers between devices, shifted(): lax.ppermute(shard, axis, [(i, (i + by) % length) for i in range(length)])  37.5 us
    reduce_sum x6, other arithmetic, axis_rows(): return jnp.sum(delta_weights(fraction)[:, :, None] * hits, axis=0)  37 us
    unnamed x85, local copies, waits for them, and re-layouts  34.9 us
    ppermute x24, waiting for transfers between devices, shifted(): lax.ppermute(shard, axis, [(i, (i + by) % length) for i in range(length)])  18.5 us
    reduce_sum x24, other arithmetic, one_axis_at_a_time(): shard = jnp.sum(lax.all_gather(shard, axis), axis=0)  14.8 us
    ppermute x3, waiting for transfers between devices, extended(): lax.ppermute(tail, axis, [(i, (i + 1) % count) for i in range(count)])  8.6 us
  transfers between devices with their start and end apart: 30, of which 15 were waited for; matrix products, arithmetic and copies ran while one was open for 12% of the time, Pallas kernels for 0%

profile of v1, /device:TPU:2, one launch (start us, length us, event | category | flops | bytes accessed | tf_op | source)
XLA Modules:
  0.0 369.1 jit_solution(14225757838168493013)
XLA Ops:
  1.5 1.9 collective-permute-start.13
  3.4 4.0 %collective-permute-start.12 = (f32[1,6,256]{2,1,0:T(8,128)S(1)}, f32[1,6,256]{2,1,0:T(8,128)S(1)}, u32[]{:S(2)}, u32[]{:S(2)}) collective-permute-start(f32[1,6,256]{2,1,0:T(8,128)S(1)} %maximum_bitcast_fusion), channel_id=1, source_target_pairs={{0,224},{32,0},{64,32},{96,64},{128,96},{160,128},{192,160},{224,1... | collective-permute-start | bytes 18440 | tf_op jit(solution)/shard_map/ppermute | solution.py:14
  9.1 3.2 collective-permute-start.1
  16.4 2.9 collective-permute-start.14
  19.4 1.5 collective-permute-done.14
  20.9 1.6 collective-permute-start.17
  24.2 2.9 collective-permute-start.3
  30.0 34.5 %select_reduce_fusion = f32[6912,134]{0,1:T(8,128)S(1)} fusion(f32[4,6912]{1,0:T(4,128)S(1)} %pad_maximum_fusion.5, s32[4,6912]{1,0:T(4,128)S(1)} %add_add_fusion), kind=kLoop, calls=%fused_computation.6 | loop fusion | flops 10188288 | bytes 3926016 | tf_op jit(solution)/shard_map/reduce_sum | solution.py:70
  66.2 1.6 collective-permute-start.4
  69.3 8.6 %collective-permute-done.4 = f32[4,14,14,3]{3,2,1,0:T(8,128)S(1)} collective-permute-done((f32[4,14,14,3]{3,2,1,0:T(8,128)S(1)}, f32[4,14,14,3]{3,2,1,0:T(8,128)S(1)}, u32[]{:S(2)}, u32[]{:S(2)}) %collective-permute-start.4) | collective-permute-done | bytes 9440 | tf_op jit(solution)/shard_map/ppermute | solution.py:24
  80.3 3.2 collective-permute-start.6
  83.5 1.6 collective-permute-done.7
  85.1 2.9 collective-permute-start.8
  88.1 1.4 collective-permute-done.8
  90.6 1.7 collective-permute-start.11
  92.3 1.5 collective-permute-done.10
  93.8 2.3 collective-permute-done.11
  96.2 14.8 %fusion.15 = f32[3,14,14,134]{3,2,1,0:T(8,128)S(1)} fusion(f32[6912,134]{0,1:T(8,128)S(1)} %select_reduce_fusion, f32[14,6912]{1,0:T(8,128)S(1)} %bitcast.106, f32[3,14,6912]{2,1,0:T(8,128)S(1)} %broadcast_multiply_fusion.2, f32[14,14,134]{2,1,0:T(8,128)S(1)} %slice_bitcast_fusion), kind=kOutput, calls=%fused_computation.21 | convolution fusion | flops 6539466752 | bytes 5673344 | tf_op jit(solution)/shard_map/cxym,mz->cxyz/dot_general | solution.py:83
  115.2 1.7 fusion.31
  120.6 17.3 %all-reduce.26 = (f32[8]{0:T(128)S(1)}, f32[8]{0:T(128)S(1)}) all-reduce(f32[8]{0:T(128)S(1)} %dynamic-update-slice, f32[8]{0:T(128)S(1)} %dynamic-update-slice.4), channel_id=1, replica_groups=mesh['gx'=8,'gy_0'=4,'gy_1'=2,'gz'=4] {'gx'}, use_global_device_ids=true, to_apply=%add | all-reduce | flops 16 | bytes 128
  142.5 9.6 %all-reduce.32 = (f32[4]{0:T(128)S(1)}, f32[4]{0:T(128)S(1)}) all-reduce(f32[4]{0:T(128)S(1)} %dynamic-update-slice.1, f32[4]{0:T(128)S(1)} %dynamic-update-slice.5), channel_id=1, replica_groups=mesh['gx'=8,'gy_0'=4,'gy_1'=2,'gz'=4] {'gy_0'}, use_global_device_ids=true, to_apply=%add.1 | all-reduce | flops 8 | bytes 64
  156.6 2.4 all-reduce.35
  160.3 1.4 dynamic-update-slice.7
  163.1 11.1 %all-reduce.29 = (f32[4]{0:T(128)S(1)}, f32[4]{0:T(128)S(1)}) all-reduce(f32[4]{0:T(128)S(1)} %dynamic-update-slice.3, f32[4]{0:T(128)S(1)} %dynamic-update-slice.7), channel_id=1, replica_groups=mesh['gx'=8,'gy_0'=4,'gy_1'=2,'gz'=4] {'gz'}, use_global_device_ids=true, to_apply=%add.3 | all-reduce | flops 8 | bytes 64
  177.0 3.2 collective-permute-start.18
  180.2 1.6 collective-permute-done.19
  181.8 2.9 collective-permute-start.20
  184.8 1.4 collective-permute-done.20
  186.7 2.0 collective-permute-start.23
  188.7 1.9 collective-permute-done.22
  190.8 16.8 %fusion.20 = f32[3,14,14,134]{3,2,1,0:T(8,128)S(1)} fusion(f32[6912,134]{0,1:T(8,128)} %copy-done, f32[3,14,6912]{2,1,0:T(8,128)S(1)} %broadcast_multiply_fusion.1, f32[14,6912]{1,0:T(8,128)S(1)} %bitcast.107, f32[14,14,134]{2,1,0:T(8,128)S(1)} %slice_bitcast_fusion), kind=kOutput, calls=%fused_computation.22 | convolution fusion | flops 6539466752 | bytes 5673344 | tf_op jit(solution)/shard_map/cxym,mz->cxyz/dot_general | solution.py:83
  211.8 1.7 fusion.32
  216.7 17.3 %all-reduce.25 = (f32[8]{0:T(128)S(1)}, f32[8]{0:T(128)S(1)}) all-reduce(f32[8]{0:T(128)S(1)} %dynamic-update-slice.8, f32[8]{0:T(128)S(1)} %dynamic-update-slice.12), channel_id=1, replica_groups=mesh['gx'=8,'gy_0'=4,'gy_1'=2,'gz'=4] {'gx'}, use_global_device_ids=true, to_apply=%add.8 | all-reduce | flops 16 | bytes 128
  237.8 7.7 %all-reduce.31 = (f32[4]{0:T(128)S(1)}, f32[4]{0:T(128)S(1)}) all-reduce(f32[4]{0:T(128)S(1)} %dynamic-update-slice.9, f32[4]{0:T(128)S(1)} %dynamic-update-slice.13), channel_id=1, replica_groups=mesh['gx'=8,'gy_0'=4,'gy_1'=2,'gz'=4] {'gy_0'}, use_global_device_ids=true, to_apply=%add.9 | all-reduce | flops 8 | bytes 64
  249.3 2.4 all-reduce.34
  255.5 10.8 %all-reduce.28 = (f32[4]{0:T(128)S(1)}, f32[4]{0:T(128)S(1)}) all-reduce(f32[4]{0:T(128)S(1)} %dynamic-update-slice.11, f32[4]{0:T(128)S(1)} %dynamic-update-slice.15), channel_id=1, replica_groups=mesh['gx'=8,'gy_0'=4,'gy_1'=2,'gz'=4] {'gz'}, use_global_device_ids=true, to_apply=%add.11 | all-reduce | flops 8 | bytes 64
  272.2 3.2 collective-permute-start.24
  275.4 1.6 collective-permute-done.25
  277.0 2.9 collective-permute-start.26
  280.0 1.4 collective-permute-done.26
  281.7 2.0 collective-permute-start.29
  283.7 2.2 collective-permute-done.28
  286.1 16.9 %fusion.25 = f32[3,14,14,134]{3,2,1,0:T(8,128)S(1)} fusion(f32[6912,134]{0,1:T(8,128)} %copy-done, f32[3,14,6912]{2,1,0:T(8,128)S(1)} %broadcast_multiply_fusion, f32[14,6912]{1,0:T(8,128)S(1)} %bitcast.108, f32[14,14,134]{2,1,0:T(8,128)S(1)} %slice_bitcast_fusion), kind=kOutput, calls=%fused_computation.23 | convolution fusion | flops 6539466752 | bytes 5673344 | tf_op jit(solution)/shard_map/cxym,mz->cxyz/dot_general | solution.py:83
  307.2 1.8 fusion.33
  312.3 17.4 %all-reduce.24 = (f32[8]{0:T(128)S(1)}, f32[8]{0:T(128)S(1)}) all-reduce(f32[8]{0:T(128)S(1)} %dynamic-update-slice.16, f32[8]{0:T(128)S(1)} %dynamic-update-slice.20), channel_id=1, replica_groups=mesh['gx'=8,'gy_0'=4,'gy_1'=2,'gz'=4] {'gx'}, use_global_device_ids=true, to_apply=%add.16 | all-reduce | flops 16 | bytes 128
  333.5 8.2 %all-reduce.30 = (f32[4]{0:T(128)S(1)}, f32[4]{0:T(128)S(1)}) all-reduce(f32[4]{0:T(128)S(1)} %dynamic-update-slice.17, f32[4]{0:T(128)S(1)} %dynamic-update-slice.21), channel_id=1, replica_groups=mesh['gx'=8,'gy_0'=4,'gy_1'=2,'gz'=4] {'gy_0'}, use_global_device_ids=true, to_apply=%add.17 | all-reduce | flops 8 | bytes 64
  345.6 2.4 all-reduce.33
  352.0 10.8 %all-reduce.27 = (f32[4]{0:T(128)S(1)}, f32[4]{0:T(128)S(1)}) all-reduce(f32[4]{0:T(128)S(1)} %dynamic-update-slice.19, f32[4]{0:T(128)S(1)} %dynamic-update-slice.23), channel_id=1, replica_groups=mesh['gx'=8,'gy_0'=4,'gy_1'=2,'gz'=4] {'gz'}, use_global_device_ids=true, to_apply=%add.19 | all-reduce | flops 8 | bytes 64
  (239 shorter events, 80.8 us)
Async XLA Ops:
  1.5 14.9 %collective-permute-start.13 = (f32[1,6,256]{2,1,0:T(8,128)S(1)}, f32[1,6,256]{2,1,0:T(8,128)S(1)}, u32[]{:S(2)}, u32[]{:S(2)}) collective-permute-start(f32[1,6,256]{2,1,0:T(8,128)S(1)} %maximum_bitcast_fusion), channel_id=1, source_target_pairs={{0,32},{32,64},{64,96},{96,128},{128,160},{160,192},{192,224},{224... | collective-permute-start | bytes 18440 | tf_op jit(solution)/shard_map/ppermute | solution.py:14
  3.4 13.0 %collective-permute-start.12 = (f32[1,6,256]{2,1,0:T(8,128)S(1)}, f32[1,6,256]{2,1,0:T(8,128)S(1)}, u32[]{:S(2)}, u32[]{:S(2)}) collective-permute-start(f32[1,6,256]{2,1,0:T(8,128)S(1)} %maximum_bitcast_fusion), channel_id=1, source_target_pairs={{0,224},{32,0},{64,32},{96,64},{128,96},{160,128},{192,160},{224,1... | collective-permute-start | bytes 18440 | tf_op jit(solution)/shard_map/ppermute | solution.py:14
  9.0 14.2 %collective-permute-start = (f32[4,3,8,128]{3,2,1,0:T(8,128)S(1)}, f32[4,3,8,128]{3,2,1,0:T(8,128)S(1)}, u32[]{:S(2)}, u32[]{:S(2)}) collective-permute-start(f32[4,3,8,128]{3,2,1,0:T(8,128)S(1)} %get-tuple-element.221), channel_id=1, source_target_pairs={{0,32},{32,64},{64,96},{96,128},{128,160},{160,192},{192,224},{224... | collective-permute-start | bytes 147464 | tf_op jit(solution)/shard_map/ppermute | solution.py:24
  9.1 14.1 %collective-permute-start.1 = (f32[4,3,8,128]{3,2,1,0:T(8,128)S(1)}, f32[4,3,8,128]{3,2,1,0:T(8,128)S(1)}, u32[]{:S(2)}, u32[]{:S(2)}) collective-permute-start(f32[4,3,8,128]{3,2,1,0:T(8,128)S(1)} %get-tuple-element.222), channel_id=1, source_target_pairs={{32,0},{64,32},{96,64},{128,96},{160,128},{192,160},{224,192},{0,2... | collective-permute-start | bytes 147464 | tf_op jit(solution)/shard_map/ppermute | solution.py:26
  16.4 4.5 %collective-permute-start.15 = (f32[3,6,256]{2,1,0:T(8,128)S(1)}, f32[3,6,256]{2,1,0:T(8,128)S(1)}, u32[]{:S(2)}, u32[]{:S(2)}) collective-permute-start(f32[3,6,256]{2,1,0:T(8,128)S(1)} %pad_maximum_fusion.8), channel_id=1, source_target_pairs={{0,4},{4,8},{8,12},{12,16},{16,20},{20,24},{24,28},{28,0},{1,5},{5... | collective-permute-start | bytes 55304 | tf_op jit(solution)/shard_map/ppermute | solution.py:14
  16.4 4.5 %collective-permute-start.14 = (f32[3,6,256]{2,1,0:T(8,128)S(1)}, f32[3,6,256]{2,1,0:T(8,128)S(1)}, u32[]{:S(2)}, u32[]{:S(2)}) collective-permute-start(f32[3,6,256]{2,1,0:T(8,128)S(1)} %pad_maximum_fusion.8), channel_id=1, source_target_pairs={{0,28},{4,0},{8,4},{12,8},{16,12},{20,16},{24,20},{28,24},{1,29},{... | collective-permute-start | bytes 55304 | tf_op jit(solution)/shard_map/ppermute | solution.py:14
  20.9 6.3 %collective-permute-start.17 = (f32[9,6,256]{2,1,0:T(8,128)S(1)}, f32[9,6,256]{2,1,0:T(8,128)S(1)}, u32[]{:S(2)}, u32[]{:S(2)}) collective-permute-start(f32[9,6,256]{2,1,0:T(8,128)S(1)} %get-tuple-element.238), channel_id=1, source_target_pairs={{0,1},{1,2},{2,3},{3,0},{4,5},{5,6},{6,7},{7,4},{8,9},{9,10},{10,1... | collective-permute-start | bytes 165896 | tf_op jit(solution)/shard_map/ppermute | solution.py:14
  22.5 4.7 %collective-permute-start.16 = (f32[9,6,256]{2,1,0:T(8,128)S(1)}, f32[9,6,256]{2,1,0:T(8,128)S(1)}, u32[]{:S(2)}, u32[]{:S(2)}) collective-permute-start(f32[9,6,256]{2,1,0:T(8,128)S(1)} %get-tuple-element.238), channel_id=1, source_target_pairs={{0,3},{1,0},{2,1},{3,2},{4,7},{5,4},{6,5},{7,6},{8,11},{9,8},{10,9... | collective-permute-start | bytes 165896 | tf_op jit(solution)/shard_map/ppermute | solution.py:14
  24.2 41.7 %collective-permute-start.2 = (f32[4,14,3,128]{3,2,1,0:T(4,128)S(1)}, f32[4,14,3,128]{3,2,1,0:T(4,128)S(1)}, u32[]{:S(2)}, u32[]{:S(2)}) collective-permute-start(f32[4,14,3,128]{3,2,1,0:T(4,128)S(1)} %get-tuple-element.183), channel_id=1, source_target_pairs={{0,4},{4,8},{8,12},{12,16},{16,20},{20,24},{24,28},{28,0},{1,5},{5... | collective-permute-start | bytes 258056 | tf_op jit(solution)/shard_map/ppermute | solution.py:24
  24.2 41.6 %collective-permute-start.3 = (f32[4,14,3,128]{3,2,1,0:T(4,128)S(1)}, f32[4,14,3,128]{3,2,1,0:T(4,128)S(1)}, u32[]{:S(2)}, u32[]{:S(2)}) collective-permute-start(f32[4,14,3,128]{3,2,1,0:T(4,128)S(1)} %get-tuple-element.184), channel_id=1, source_target_pairs={{4,0},{8,4},{12,8},{16,12},{20,16},{24,20},{28,24},{0,28},{5,1},{9... | collective-permute-start | bytes 258056 | tf_op jit(solution)/shard_map/ppermute | solution.py:26
  27.2 38.7 %copy-start.1 = (f32[3,8,8,128]{3,2,1,0:T(8,128)S(1)}, f32[3,8,8,128]{3,2,1,0:T(8,128)}, u32[]{:S(2)}) copy-start(f32[3,8,8,128]{3,2,1,0:T(8,128)} %param.10) | copy-start | bytes 294916
  64.6 31.6 %copy-start = (f32[6912,134]{0,1:T(8,128)}, f32[6912,134]{0,1:T(8,128)S(1)}, u32[]{:S(2)}) copy-start(f32[6912,134]{0,1:T(8,128)S(1)} %select_reduce_fusion) | copy-start | bytes 11114500
  64.8 15.4 %copy-start.3 = (f32[3,256]{1,0:T(4,128)S(1)}, f32[3,256]{1,0:T(4,128)}, u32[]{:S(2)}) copy-start(f32[3,256]{1,0:T(4,128)} %param.13) | copy-start | bytes 9220
  66.2 11.7 %collective-permute-start.4 = (f32[4,14,14,3]{3,2,1,0:T(8,128)S(1)}, f32[4,14,14,3]{3,2,1,0:T(8,128)S(1)}, u32[]{:S(2)}, u32[]{:S(2)}) collective-permute-start(f32[4,14,14,3]{3,2,1,0:T(8,128)S(1)} %get-tuple-element.181), channel_id=1, source_target_pairs={{0,1},{1,2},{2,3},{3,0},{4,5},{5,6},{6,7},{7,4},{8,9},{9,10},{10,1... | collective-permute-start | bytes 28232 | tf_op jit(solution)/shard_map/ppermute | solution.py:24
  67.7 11.1 %collective-permute-start.5 = (f32[4,14,14,3]{3,2,1,0:T(8,128)S(1)}, f32[4,14,14,3]{3,2,1,0:T(8,128)S(1)}, u32[]{:S(2)}, u32[]{:S(2)}) collective-permute-start(f32[4,14,14,3]{3,2,1,0:T(8,128)S(1)} %get-tuple-element.182), channel_id=1, source_target_pairs={{1,0},{2,1},{3,2},{0,3},{5,4},{6,5},{7,6},{4,7},{9,8},{10,9},{11,1... | collective-permute-start | bytes 28232 | tf_op jit(solution)/shard_map/ppermute | solution.py:26
  80.2 4.9 %collective-permute-start.7 = (f32[1,3,256]{2,1,0:T(4,128)S(1)}, f32[1,3,256]{2,1,0:T(4,128)S(1)}, u32[]{:S(2)}, u32[]{:S(2)}) collective-permute-start(f32[1,3,256]{2,1,0:T(4,128)S(1)} %bitcast.109), channel_id=1, source_target_pairs={{0,32},{32,64},{64,96},{96,128},{128,160},{160,192},{192,224},{224... | collective-permute-start | bytes 9224 | tf_op jit(solution)/shard_map/ppermute | solution.py:14
  80.3 4.8 %collective-permute-start.6 = (f32[1,3,256]{2,1,0:T(4,128)S(1)}, f32[1,3,256]{2,1,0:T(4,128)S(1)}, u32[]{:S(2)}, u32[]{:S(2)}) collective-permute-start(f32[1,3,256]{2,1,0:T(4,128)S(1)} %bitcast.110), channel_id=1, source_target_pairs={{0,224},{32,0},{64,32},{96,64},{128,96},{160,128},{192,160},{224,1... | collective-permute-start | bytes 9224 | tf_op jit(solution)/shard_map/ppermute | solution.py:14
  85.1 4.4 %collective-permute-start.9 = (f32[3,3,256]{2,1,0:T(4,128)S(1)}, f32[3,3,256]{2,1,0:T(4,128)S(1)}, u32[]{:S(2)}, u32[]{:S(2)}) collective-permute-start(f32[3,3,256]{2,1,0:T(4,128)S(1)} %pad_maximum_fusion.9), channel_id=1, source_target_pairs={{0,4},{4,8},{8,12},{12,16},{16,20},{20,24},{24,28},{28,0},{1,5},{5... | collective-permute-start | bytes 27656 | tf_op jit(solution)/shard_map/ppermute | solution.py:14
  85.1 4.3 %collective-permute-start.8 = (f32[3,3,256]{2,1,0:T(4,128)S(1)}, f32[3,3,256]{2,1,0:T(4,128)S(1)}, u32[]{:S(2)}, u32[]{:S(2)}) collective-permute-start(f32[3,3,256]{2,1,0:T(4,128)S(1)} %pad_maximum_fusion.9), channel_id=1, source_target_pairs={{0,28},{4,0},{8,4},{12,8},{16,12},{20,16},{24,20},{28,24},{1,29},{... | collective-permute-start | bytes 27656 | tf_op jit(solution)/shard_map/ppermute | solution.py:14
  89.5 4.3 %collective-permute-start.10 = (f32[9,3,256]{2,1,0:T(4,128)S(1)}, f32[9,3,256]{2,1,0:T(4,128)S(1)}, u32[]{:S(2)}, u32[]{:S(2)}) collective-permute-start(f32[9,3,256]{2,1,0:T(4,128)S(1)} %get-tuple-element.250), channel_id=1, source_target_pairs={{0,3},{1,0},{2,1},{3,2},{4,7},{5,4},{6,5},{7,6},{8,11},{9,8},{10,9... | collective-permute-start | bytes 82952 | tf_op jit(solution)/shard_map/ppermute | solution.py:14
  90.6 5.5 %collective-permute-start.11 = (f32[9,3,256]{2,1,0:T(4,128)S(1)}, f32[9,3,256]{2,1,0:T(4,128)S(1)}, u32[]{:S(2)}, u32[]{:S(2)}) collective-permute-start(f32[9,3,256]{2,1,0:T(4,128)S(1)} %get-tuple-element.250), channel_id=1, source_target_pairs={{0,1},{1,2},{2,3},{3,0},{4,5},{5,6},{6,7},{7,4},{8,9},{9,10},{10,1... | collective-permute-start | bytes 82952 | tf_op jit(solution)/shard_map/ppermute | solution.py:14
  115.1 1.8 copy-start.2
  115.1 4.9 %copy-start.6 = (u32[256]{0:T(256)S(1)}, u32[256]{0:T(256)}, u32[]{:S(2)}) copy-start(u32[256]{0:T(256)} %constant.199) | copy-start | bytes 3076
  115.1 26.7 %copy-start.5 = (u32[256]{0:T(256)S(1)}, u32[256]{0:T(256)}, u32[]{:S(2)}) copy-start(u32[256]{0:T(256)} %constant.204) | copy-start | bytes 3076
  115.2 40.8 %copy-start.4 = (u32[256]{0:T(256)S(1)}, u32[256]{0:T(256)}, u32[]{:S(2)}) copy-start(u32[256]{0:T(256)} %constant.209) | copy-start | bytes 3076
  176.9 4.9 %collective-permute-start.19 = (f32[1,3,256]{2,1,0:T(4,128)S(1)}, f32[1,3,256]{2,1,0:T(4,128)S(1)}, u32[]{:S(2)}, u32[]{:S(2)}) collective-permute-start(f32[1,3,256]{2,1,0:T(4,128)S(1)} %bitcast.112), channel_id=1, source_target_pairs={{0,32},{32,64},{64,96},{96,128},{128,160},{160,192},{192,224},{224... | collective-permute-start | bytes 9224 | tf_op jit(solution)/shard_map/ppermute | solution.py:14
  177.0 4.8 %collective-permute-start.18 = (f32[1,3,256]{2,1,0:T(4,128)S(1)}, f32[1,3,256]{2,1,0:T(4,128)S(1)}, u32[]{:S(2)}, u32[]{:S(2)}) collective-permute-start(f32[1,3,256]{2,1,0:T(4,128)S(1)} %bitcast.113), channel_id=1, source_target_pairs={{0,224},{32,0},{64,32},{96,64},{128,96},{160,128},{192,160},{224,1... | collective-permute-start | bytes 9224 | tf_op jit(solution)/shard_map/ppermute | solution.py:14
  181.8 4.4 %collective-permute-start.21 = (f32[3,3,256]{2,1,0:T(4,128)S(1)}, f32[3,3,256]{2,1,0:T(4,128)S(1)}, u32[]{:S(2)}, u32[]{:S(2)}) collective-permute-start(f32[3,3,256]{2,1,0:T(4,128)S(1)} %pad_maximum_fusion.10), channel_id=1, source_target_pairs={{0,4},{4,8},{8,12},{12,16},{16,20},{20,24},{24,28},{28,0},{1,5},{5... | collective-permute-start | bytes 27656 | tf_op jit(solution)/shard_map/ppermute | solution.py:14
  181.8 4.3 %collective-permute-start.20 = (f32[3,3,256]{2,1,0:T(4,128)S(1)}, f32[3,3,256]{2,1,0:T(4,128)S(1)}, u32[]{:S(2)}, u32[]{:S(2)}) collective-permute-start(f32[3,3,256]{2,1,0:T(4,128)S(1)} %pad_maximum_fusion.10), channel_id=1, source_target_pairs={{0,28},{4,0},{8,4},{12,8},{16,12},{20,16},{24,20},{28,24},{1,29},{... | collective-permute-start | bytes 27656 | tf_op jit(solution)/shard_map/ppermute | solution.py:14
  186.2 4.4 %collective-permute-start.22 = (f32[9,3,256]{2,1,0:T(4,128)S(1)}, f32[9,3,256]{2,1,0:T(4,128)S(1)}, u32[]{:S(2)}, u32[]{:S(2)}) collective-permute-start(f32[9,3,256]{2,1,0:T(4,128)S(1)} %get-tuple-element.246), channel_id=1, source_target_pairs={{0,3},{1,0},{2,1},{3,2},{4,7},{5,4},{6,5},{7,6},{8,11},{9,8},{10,9... | collective-permute-start | bytes 82952 | tf_op jit(solution)/shard_map/ppermute | solution.py:14
  186.7 4.0 %collective-permute-start.23 = (f32[9,3,256]{2,1,0:T(4,128)S(1)}, f32[9,3,256]{2,1,0:T(4,128)S(1)}, u32[]{:S(2)}, u32[]{:S(2)}) collective-permute-start(f32[9,3,256]{2,1,0:T(4,128)S(1)} %get-tuple-element.246), channel_id=1, source_target_pairs={{0,1},{1,2},{2,3},{3,0},{4,5},{5,6},{6,7},{7,4},{8,9},{9,10},{10,1... | collective-permute-start | bytes 82952 | tf_op jit(solution)/shard_map/ppermute | solution.py:14
  272.1 4.9 %collective-permute-start.25 = (f32[1,3,256]{2,1,0:T(4,128)S(1)}, f32[1,3,256]{2,1,0:T(4,128)S(1)}, u32[]{:S(2)}, u32[]{:S(2)}) collective-permute-start(f32[1,3,256]{2,1,0:T(4,128)S(1)} %bitcast.121), channel_id=1, source_target_pairs={{0,32},{32,64},{64,96},{96,128},{128,160},{160,192},{192,224},{224... | collective-permute-start | bytes 9224 | tf_op jit(solution)/shard_map/ppermute | solution.py:14
  272.2 4.8 %collective-permute-start.24 = (f32[1,3,256]{2,1,0:T(4,128)S(1)}, f32[1,3,256]{2,1,0:T(4,128)S(1)}, u32[]{:S(2)}, u32[]{:S(2)}) collective-permute-start(f32[1,3,256]{2,1,0:T(4,128)S(1)} %bitcast.122), channel_id=1, source_target_pairs={{0,224},{32,0},{64,32},{96,64},{128,96},{160,128},{192,160},{224,1... | collective-permute-start | bytes 9224 | tf_op jit(solution)/shard_map/ppermute | solution.py:14
  277.0 4.4 %collective-permute-start.27 = (f32[3,3,256]{2,1,0:T(4,128)S(1)}, f32[3,3,256]{2,1,0:T(4,128)S(1)}, u32[]{:S(2)}, u32[]{:S(2)}) collective-permute-start(f32[3,3,256]{2,1,0:T(4,128)S(1)} %pad_maximum_fusion.11), channel_id=1, source_target_pairs={{0,4},{4,8},{8,12},{12,16},{16,20},{20,24},{24,28},{28,0},{1,5},{5... | collective-permute-start | bytes 27656 | tf_op jit(solution)/shard_map/ppermute | solution.py:14
  277.0 4.3 %collective-permute-start.26 = (f32[3,3,256]{2,1,0:T(4,128)S(1)}, f32[3,3,256]{2,1,0:T(4,128)S(1)}, u32[]{:S(2)}, u32[]{:S(2)}) collective-permute-start(f32[3,3,256]{2,1,0:T(4,128)S(1)} %pad_maximum_fusion.11), channel_id=1, source_target_pairs={{0,28},{4,0},{8,4},{12,8},{16,12},{20,16},{24,20},{28,24},{1,29},{... | collective-permute-start | bytes 27656 | tf_op jit(solution)/shard_map/ppermute | solution.py:14
  281.4 4.6 %collective-permute-start.28 = (f32[9,3,256]{2,1,0:T(4,128)S(1)}, f32[9,3,256]{2,1,0:T(4,128)S(1)}, u32[]{:S(2)}, u32[]{:S(2)}) collective-permute-start(f32[9,3,256]{2,1,0:T(4,128)S(1)} %get-tuple-element.242), channel_id=1, source_target_pairs={{0,3},{1,0},{2,1},{3,2},{4,7},{5,4},{6,5},{7,6},{8,11},{9,8},{10,9... | collective-permute-start | bytes 82952 | tf_op jit(solution)/shard_map/ppermute | solution.py:14
  281.7 4.3 %collective-permute-start.29 = (f32[9,3,256]{2,1,0:T(4,128)S(1)}, f32[9,3,256]{2,1,0:T(4,128)S(1)}, u32[]{:S(2)}, u32[]{:S(2)}) collective-permute-start(f32[9,3,256]{2,1,0:T(4,128)S(1)} %get-tuple-element.242), channel_id=1, source_target_pairs={{0,1},{1,2},{2,3},{3,0},{4,5},{5,6},{6,7},{7,4},{8,9},{9,10},{10,1... | collective-permute-start | bytes 82952 | tf_op jit(solution)/shard_map/ppermute | solution.py:14
